TPU v7x, 32 devices: a whole 2x2x4 slice. The times are simulated.
32 devices in a mesh: groups: 1, seq: 32 (over z, y, x, core).
Axes of the slice: x: 2, y: 2, z: 4, core: 2. Of those that a mesh axis runs over, the one named last changes fastest.
Arguments:
- queries: bfloat16 [4096, 4096], P(('groups', 'seq')), may hold values from -100 to 100
- keys_values: bfloat16 [4096, 2, 512], P(('groups', 'seq')), may hold values from -5 to 5
- head_signs: int32 [32, 128], replicated, may hold values from -1 to 1, as said below
- out_codes: int32 [512, 8192], P(None, 'seq'), may hold values from -2147483648 to 2147483647, as said below
- out_scales: bfloat16 [32, 8192], replicated, may hold values from 0.019897461 to 0.19921875
Outputs:
- projected: bfloat16 [4096, 8192], P(('groups', 'seq'))
Inputs may be any that keep to these rules, and one draw needn't show every extreme that they name: `head_signs`: every entry is -1 or 1. `out_codes`: each word holds eight codes of 0 to 15, the code of row 8 i + k in bits 4k to 4k + 3 of word row i, the word read as a signed 32-bit integer.
All inputs are finite; a program needn't handle non-finite values.
Results may differ from a plain program's by a relative error of at most 0.006.
Values may be sent and summed in bfloat16 or wider, within the bound.
A program may use at most 128 MiB of HBM per device.

v0:
```python
import math

import jax
import jax.numpy as jnp
from jax import lax
from jax.sharding import PartitionSpec as P

HEADS = 32
KV = 4
HD = 128
GROUP = 128
WINDOW = 2048


def passed_along(block, axis, distance):
    devices = range(lax.axis_size(axis))
    route = [(i - distance, i) for i in devices if i - distance in devices]
    return lax.ppermute(block, axis, route)


def hadamard(order):
    index = jnp.arange(order, dtype=jnp.int32)
    common = jnp.bitwise_and(index[:, None], index[None, :])
    ones = jnp.zeros((order, order), jnp.int32)
    for bit_index in range(order.bit_length()):
        ones = ones + jnp.bitwise_and(jnp.right_shift(common, bit_index), 1)
    return jnp.where(ones % 2 == 0, 1.0, -1.0).astype(jnp.float32)


def project(inputs, code_words, scale_cols):
    word_rows = code_words.shape[0]
    columns = code_words.shape[1]
    tok_rows = inputs.shape[0]
    group_words = GROUP // 8
    scale_rows = scale_cols.shape[0]
    tile_width = math.gcd(columns, 512)
    tile_count = columns // tile_width
    input_classes = jnp.transpose(inputs.reshape(tok_rows, word_rows, 8), (2, 0, 1))

    def one_tile(tile_index, output):
        begin = (tile_index * tile_width).astype(jnp.int32)
        tile_words = lax.dynamic_slice_in_dim(code_words, begin, tile_width, 1)
        tile_scales = lax.dynamic_slice_in_dim(scale_cols, begin, tile_width, 1).astype(jnp.float32)
        total = jnp.zeros((tok_rows, tile_width), jnp.float32)
        for nibble_index in range(8):
            code_vals = (
                jnp.bitwise_and(jnp.right_shift(tile_words, 4 * nibble_index), 15) - 8
            ).astype(jnp.float32)
            scaled = (
                code_vals.reshape(scale_rows, group_words, tile_width) * tile_scales[:, None, :]
            )
            weight = scaled.reshape(word_rows, tile_width).astype(jnp.bfloat16)
            total = total + jnp.dot(
                input_classes[nibble_index], weight, preferred_element_type=jnp.float32
            )
        return lax.dynamic_update_slice(output, total, (jnp.zeros((), jnp.int32), begin))

    initial = jnp.zeros((tok_rows, columns), jnp.float32)
    return lax.fori_loop(0, tile_count, one_tile, initial)


def on_device(queries, keys_values, head_signs, out_codes, out_scales):
    tok_rows = queries.shape[0]
    reach_blocks = (WINDOW + tok_rows - 2) // tok_rows
    my_start = lax.axis_index("seq") * tok_rows
    blocks = []
    current = keys_values
    for distance in range(reach_blocks):
        current = passed_along(current, "seq", 1)
        blocks.insert(0, current)
    window = jnp.concatenate(blocks + [keys_values], axis=0)
    key_count = window.shape[0]
    key_pos = my_start - reach_blocks * tok_rows + jnp.arange(key_count, dtype=jnp.int32)
    query_pos = my_start + jnp.arange(tok_rows, dtype=jnp.int32)
    distance_grid = query_pos[:, None] - key_pos[None, :]
    allowed = (distance_grid >= 0) & (distance_grid < WINDOW) & (key_pos[None, :] >= 0)
    allowed = allowed[None]
    per_group = HEADS // KV
    query_groups = jnp.transpose(queries.reshape(tok_rows, KV, per_group, HD), (1, 0, 2, 3))
    key_groups = jnp.transpose(window[:, 0].reshape(key_count, KV, HD), (1, 0, 2))
    value_groups = jnp.transpose(window[:, 1].reshape(key_count, KV, HD), (1, 0, 2))

    def attend(items):
        query_rows, key_rows, value_rows = items
        scores = jnp.einsum(
            "ihd,jd->hij", query_rows, key_rows, preferred_element_type=jnp.float32
        ) / math.sqrt(HD)
        scores = jnp.where(allowed, scores, -jnp.inf)
        row_max = jnp.max(scores, axis=-1, keepdims=True)
        weights = jnp.where(allowed, jnp.exp(scores - row_max), 0.0)
        total = jnp.sum(weights, axis=-1, keepdims=True)
        rounded = weights.astype(jnp.bfloat16)
        weighted = (
            jnp.einsum("hij,jd->hid", rounded, value_rows, preferred_element_type=jnp.float32)
            / total
        )
        return jnp.transpose(weighted, (1, 0, 2))

    attended = lax.map(attend, (query_groups, key_groups, value_groups))
    attended = jnp.transpose(attended, (1, 0, 2, 3)).reshape(tok_rows, HEADS, HD)
    signed = attended * head_signs.astype(jnp.float32)[None]
    mixed = jnp.einsum(
        "thd,de->the", signed, hadamard(HD), precision=lax.Precision.HIGHEST
    ) / math.sqrt(HD)
    rotated = mixed.astype(jnp.bfloat16).reshape(tok_rows, HEADS * HD)
    partial_out = project(rotated, lax.all_gather(out_codes, "seq", axis=1, tiled=True), out_scales)
    return partial_out.astype(jnp.bfloat16)


def solution(mesh):
    return jax.shard_map(
        on_device,
        mesh=mesh,
        in_specs=(
            P(("groups", "seq"), None),
            P(("groups", "seq"), None, None),
            P(),
            P(None, "seq"),
            P(),
        ),
        out_specs=P(("groups", "seq"), None),
        check_vma=False,
    )
```

profile of v0, /device:TPU:16, one launch (start us, length us, event | category | flops | bytes accessed | tf_op | source)
XLA Modules:
  0.0 400.9 jit_solution(6875257030004767151)
XLA Ops:
  10.3 7.6 %collective-permute-done = bf16[128,2,512]{0,2,1:T(8,128)(2,1)S(1)} collective-permute-done((bf16[128,2,512]{0,2,1:T(8,128)(2,1)S(1)}, bf16[128,2,512]{0,2,1:T(8,128)(2,1)S(1)}, u32[]{:S(2)}, u32[]{:S(2)}) %collective-permute-start) | collective-permute-done | bytes 262176 | tf_op jit(solution)/shard_map/ppermute | solution.py:18
  19.8 9.7 %collective-permute-done.1 = bf16[128,2,512]{0,2,1:T(8,128)(2,1)S(1)} collective-permute-done((bf16[128,2,512]{0,2,1:T(8,128)(2,1)S(1)}, bf16[128,2,512]{0,2,1:T(8,128)(2,1)S(1)}, u32[]{:S(2)}, u32[]{:S(2)}) %collective-permute-start.1) | collective-permute-done | bytes 262176 | tf_op jit(solution)/shard_map/ppermute | solution.py:18
  31.5 9.2 %collective-permute-done.2 = bf16[128,2,512]{0,2,1:T(8,128)(2,1)S(1)} collective-permute-done((bf16[128,2,512]{0,2,1:T(8,128)(2,1)S(1)}, bf16[128,2,512]{0,2,1:T(8,128)(2,1)S(1)}, u32[]{:S(2)}, u32[]{:S(2)}) %collective-permute-start.2) | collective-permute-done | bytes 262176 | tf_op jit(solution)/shard_map/ppermute | solution.py:18
  42.6 16.0 %collective-permute-done.3 = bf16[128,2,512]{0,2,1:T(8,128)(2,1)S(1)} collective-permute-done((bf16[128,2,512]{0,2,1:T(8,128)(2,1)S(1)}, bf16[128,2,512]{0,2,1:T(8,128)(2,1)S(1)}, u32[]{:S(2)}, u32[]{:S(2)}) %collective-permute-start.3) | collective-permute-done | bytes 262176 | tf_op jit(solution)/shard_map/ppermute | solution.py:18
  60.4 10.1 %collective-permute-done.4 = bf16[128,2,512]{0,2,1:T(8,128)(2,1)S(1)} collective-permute-done((bf16[128,2,512]{0,2,1:T(8,128)(2,1)S(1)}, bf16[128,2,512]{0,2,1:T(8,128)(2,1)S(1)}, u32[]{:S(2)}, u32[]{:S(2)}) %collective-permute-start.4) | collective-permute-done | bytes 262176 | tf_op jit(solution)/shard_map/ppermute | solution.py:18
  72.5 8.4 %collective-permute-done.5 = bf16[128,2,512]{0,2,1:T(8,128)(2,1)S(1)} collective-permute-done((bf16[128,2,512]{0,2,1:T(8,128)(2,1)S(1)}, bf16[128,2,512]{0,2,1:T(8,128)(2,1)S(1)}, u32[]{:S(2)}, u32[]{:S(2)}) %collective-permute-start.5) | collective-permute-done | bytes 262176 | tf_op jit(solution)/shard_map/ppermute | solution.py:18
  82.8 20.2 %collective-permute-done.6 = bf16[128,2,512]{0,2,1:T(8,128)(2,1)S(1)} collective-permute-done((bf16[128,2,512]{0,2,1:T(8,128)(2,1)S(1)}, bf16[128,2,512]{0,2,1:T(8,128)(2,1)S(1)}, u32[]{:S(2)}, u32[]{:S(2)}) %collective-permute-start.6) | collective-permute-done | bytes 262176 | tf_op jit(solution)/shard_map/ppermute | solution.py:18
  104.9 19.9 %collective-permute-done.7 = bf16[128,2,512]{0,2,1:T(8,128)(2,1)S(1)} collective-permute-done((bf16[128,2,512]{0,2,1:T(8,128)(2,1)S(1)}, bf16[128,2,512]{0,2,1:T(8,128)(2,1)S(1)}, u32[]{:S(2)}, u32[]{:S(2)}) %collective-permute-start.7) | collective-permute-done | bytes 262176 | tf_op jit(solution)/shard_map/ppermute | solution.py:18
  126.7 20.0 %collective-permute-done.8 = bf16[128,2,512]{0,2,1:T(8,128)(2,1)S(1)} collective-permute-done((bf16[128,2,512]{0,2,1:T(8,128)(2,1)S(1)}, bf16[128,2,512]{0,2,1:T(8,128)(2,1)S(1)}, u32[]{:S(2)}, u32[]{:S(2)}) %collective-permute-start.8) | collective-permute-done | bytes 262176 | tf_op jit(solution)/shard_map/ppermute | solution.py:18
  149.4 7.6 %collective-permute-done.9 = bf16[128,2,512]{0,2,1:T(8,128)(2,1)S(1)} collective-permute-done((bf16[128,2,512]{0,2,1:T(8,128)(2,1)S(1)}, bf16[128,2,512]{0,2,1:T(8,128)(2,1)S(1)}, u32[]{:S(2)}, u32[]{:S(2)}) %collective-permute-start.9) | collective-permute-done | bytes 262176 | tf_op jit(solution)/shard_map/ppermute | solution.py:18
  159.5 7.6 %collective-permute-done.10 = bf16[128,2,512]{0,2,1:T(8,128)(2,1)S(1)} collective-permute-done((bf16[128,2,512]{0,2,1:T(8,128)(2,1)S(1)}, bf16[128,2,512]{0,2,1:T(8,128)(2,1)S(1)}, u32[]{:S(2)}, u32[]{:S(2)}) %collective-permute-start.10) | collective-permute-done | bytes 262176 | tf_op jit(solution)/shard_map/ppermute | solution.py:18
  169.7 7.6 %collective-permute-done.11 = bf16[128,2,512]{0,2,1:T(8,128)(2,1)S(1)} collective-permute-done((bf16[128,2,512]{0,2,1:T(8,128)(2,1)S(1)}, bf16[128,2,512]{0,2,1:T(8,128)(2,1)S(1)}, u32[]{:S(2)}, u32[]{:S(2)}) %collective-permute-start.11) | collective-permute-done | bytes 262176 | tf_op jit(solution)/shard_map/ppermute | solution.py:18
  179.9 7.6 %collective-permute-done.12 = bf16[128,2,512]{0,2,1:T(8,128)(2,1)S(1)} collective-permute-done((bf16[128,2,512]{0,2,1:T(8,128)(2,1)S(1)}, bf16[128,2,512]{0,2,1:T(8,128)(2,1)S(1)}, u32[]{:S(2)}, u32[]{:S(2)}) %collective-permute-start.12) | collective-permute-done | bytes 262176 | tf_op jit(solution)/shard_map/ppermute | solution.py:18
  190.1 7.6 %collective-permute-done.13 = bf16[128,2,512]{0,2,1:T(8,128)(2,1)S(1)} collective-permute-done((bf16[128,2,512]{0,2,1:T(8,128)(2,1)S(1)}, bf16[128,2,512]{0,2,1:T(8,128)(2,1)S(1)}, u32[]{:S(2)}, u32[]{:S(2)}) %collective-permute-start.13) | collective-permute-done | bytes 262176 | tf_op jit(solution)/shard_map/ppermute | solution.py:18
  199.6 7.7 %collective-permute-done.14 = bf16[128,2,512]{0,2,1:T(8,128)(2,1)} collective-permute-done((bf16[128,2,512]{0,2,1:T(8,128)(2,1)S(1)}, bf16[128,2,512]{0,2,1:T(8,128)(2,1)}, u32[]{:S(2)}, u32[]{:S(2)}) %collective-permute-start.14) | collective-permute-done | bytes 262176 | tf_op jit(solution)/shard_map/ppermute | solution.py:18
  227.5 57.7 %while.28 = (s32[]{:T(128)}, f32[4,128,8,128]{3,1,2,0:T(8,128)}, bf16[4,2176,128]{1,2,0:T(8,128)(2,1)}, bf16[4,128,8,128]{1,3,2,0:T(8,128)(2,1)S(1)}, bf16[4,217...) while((s32[]{:T(128)}, f32[4,128,8,128]{3,1,2,0:T(8,128)}, ...), condition=%wide.region_3.4_spmd.clone, body=%wide.region_0.3_spmd.clone.sunk | while | flops 1155745920 | bytes 11670749 | solution.py:99
  229.9 7.6 %fusion.170 = (f32[8,128]{1,0:T(8,128)}, bf16[8,128,2176]{1,2,0:T(8,128)(2,1)}) fusion(pred[128,2176]{0,1:T(8,128)(4,1)S(1)} %fusion.169, bf16[4,2176,128]{1,2,0:T(8,128)(2,1)} %get-tuple-element.382, s32[]{:T(128)} %get-tuple-element.371, bf16[4,128,8,128]{1,3,2,0:T(8,128)(2,1)S(1)} %get-tuple-element.383), kind=kOutput, calls=%fused_computation.131.clone.1 | convolution fusion | flops 583796864 | bytes 5837824 | tf_op jit(solution)/shard_map/while/body/eval_jaxpr/sub | solution.py:90
  244.3 7.6 %fusion.170 = (f32[8,128]{1,0:T(8,128)}, bf16[8,128,2176]{1,2,0:T(8,128)(2,1)}) fusion(pred[128,2176]{0,1:T(8,128)(4,1)S(1)} %fusion.169, bf16[4,2176,128]{1,2,0:T(8,128)(2,1)} %get-tuple-element.382, s32[]{:T(128)} %get-tuple-element.371, bf16[4,128,8,128]{1,3,2,0:T(8,128)(2,1)S(1)} %get-tuple-element.383), kind=kOutput, calls=%fused_computation.131.clone.1 | convolution fusion | flops 583796864 | bytes 5837824 | tf_op jit(solution)/shard_map/while/body/eval_jaxpr/sub | solution.py:90
  251.9 4.4 %fusion.171 = f32[4,128,8,128]{3,1,2,0:T(8,128)} fusion(f32[4,128,8,128]{3,1,2,0:T(8,128)} %get-tuple-element.372, s32[]{:T(128)} %get-tuple-element.371, bf16[8,128,2176]{1,2,0:T(8,128)(2,1)} %get-tuple-element.360, bf16[4,2176,128]{1,2,0:T(8,128)(2,1)S(1)} %get-tuple-element.384, f32[128,8]{0,1:T(8,128)} %bitcast.188), kind=kOutput, calls=%fused_computation.59.clone.1 | convolution fusion | flops 570556416 | bytes 5542912 | tf_op jit(solution)/shard_map/while/body/eval_jaxpr/hij,jd->hid/dot_general | solution.py:94
  258.7 7.6 %fusion.170 = (f32[8,128]{1,0:T(8,128)}, bf16[8,128,2176]{1,2,0:T(8,128)(2,1)}) fusion(pred[128,2176]{0,1:T(8,128)(4,1)S(1)} %fusion.169, bf16[4,2176,128]{1,2,0:T(8,128)(2,1)} %get-tuple-element.382, s32[]{:T(128)} %get-tuple-element.371, bf16[4,128,8,128]{1,3,2,0:T(8,128)(2,1)S(1)} %get-tuple-element.383), kind=kOutput, calls=%fused_computation.131.clone.1 | convolution fusion | flops 583796864 | bytes 5837824 | tf_op jit(solution)/shard_map/while/body/eval_jaxpr/sub | solution.py:90
  266.4 4.4 %fusion.171 = f32[4,128,8,128]{3,1,2,0:T(8,128)} fusion(f32[4,128,8,128]{3,1,2,0:T(8,128)} %get-tuple-element.372, s32[]{:T(128)} %get-tuple-element.371, bf16[8,128,2176]{1,2,0:T(8,128)(2,1)} %get-tuple-element.360, bf16[4,2176,128]{1,2,0:T(8,128)(2,1)S(1)} %get-tuple-element.384, f32[128,8]{0,1:T(8,128)} %bitcast.188), kind=kOutput, calls=%fused_computation.59.clone.1 | convolution fusion | flops 570556416 | bytes 5542912 | tf_op jit(solution)/shard_map/while/body/eval_jaxpr/hij,jd->hid/dot_general | solution.py:94
  273.2 7.6 %fusion.170 = (f32[8,128]{1,0:T(8,128)}, bf16[8,128,2176]{1,2,0:T(8,128)(2,1)}) fusion(pred[128,2176]{0,1:T(8,128)(4,1)S(1)} %fusion.169, bf16[4,2176,128]{1,2,0:T(8,128)(2,1)} %get-tuple-element.382, s32[]{:T(128)} %get-tuple-element.371, bf16[4,128,8,128]{1,3,2,0:T(8,128)(2,1)S(1)} %get-tuple-element.383), kind=kOutput, calls=%fused_computation.131.clone.1 | convolution fusion | flops 583796864 | bytes 5837824 | tf_op jit(solution)/shard_map/while/body/eval_jaxpr/sub | solution.py:90
  280.8 4.4 %fusion.171 = f32[4,128,8,128]{3,1,2,0:T(8,128)} fusion(f32[4,128,8,128]{3,1,2,0:T(8,128)} %get-tuple-element.372, s32[]{:T(128)} %get-tuple-element.371, bf16[8,128,2176]{1,2,0:T(8,128)(2,1)} %get-tuple-element.360, bf16[4,2176,128]{1,2,0:T(8,128)(2,1)S(1)} %get-tuple-element.384, f32[128,8]{0,1:T(8,128)} %bitcast.188), kind=kOutput, calls=%fused_computation.59.clone.1 | convolution fusion | flops 570556416 | bytes 5542912 | tf_op jit(solution)/shard_map/while/body/eval_jaxpr/hij,jd->hid/dot_general | solution.py:94
  290.1 101.0 %while.27 = (s32[]{:T(128)}, bf16[128,8192]{0,1:T(8,128)(2,1)S(1)}, s32[512,8192]{1,0:T(8,128)}, bf16[32,8192]{1,0:T(8,128)(2,1)}, bf16[8,128,512]{2,1,0:T(8,128...) while((s32[]{:T(128)}, bf16[128,8192]{0,1:T(8,128)(2,1)S(1)}, s32[512,8192]{1,0:T(8,128)}, ...), condition=%wide.region_5.6_spmd, body=%wide.region_4.5_spmd.sunk | while | flops 549928960 | bytes 14581911 | solution.py:59
  (227 shorter events, 175.7 us)
Async XLA Ops:
  6.5 283.3 %all-gather.2.cloned.1.call-start = ((), (), s32[]{:S(2)}) async-start(), calls=%async_computation | async-start | bytes 17301504 | tf_op jit(solution)/shard_map/all_gather | solution.py:106
  8.4 9.5 %collective-permute-start = (bf16[128,2,512]{0,2,1:T(8,128)(2,1)S(1)}, bf16[128,2,512]{0,2,1:T(8,128)(2,1)S(1)}, u32[]{:S(2)}, u32[]{:S(2)}) collective-permute-start(bf16[128,2,512]{0,2,1:T(8,128)(2,1)S(1)} %copy.10), channel_id=1, source_target_pairs={{0,1},{1,2},{2,3},{3,4},{4,5},{5,6},{6,7},{7,8},{8,9},{9,10},{10,1... | collective-permute-start | bytes 786440 | tf_op jit(solution)/shard_map/ppermute | solution.py:18
  17.9 11.7 %collective-permute-start.1 = (bf16[128,2,512]{0,2,1:T(8,128)(2,1)S(1)}, bf16[128,2,512]{0,2,1:T(8,128)(2,1)S(1)}, u32[]{:S(2)}, u32[]{:S(2)}) collective-permute-start(bf16[128,2,512]{0,2,1:T(8,128)(2,1)S(1)} %collective-permute-done), channel_id=1, source_target_pairs={{0,1},{1,2},{2,3},{3,4},{4,5},{5,6},{6,7},{7,8},{8,9},{9,10},{10,1... | collective-permute-start | bytes 786440 | tf_op jit(solution)/shard_map/ppermute | solution.py:18
  29.5 11.1 %collective-permute-start.2 = (bf16[128,2,512]{0,2,1:T(8,128)(2,1)S(1)}, bf16[128,2,512]{0,2,1:T(8,128)(2,1)S(1)}, u32[]{:S(2)}, u32[]{:S(2)}) collective-permute-start(bf16[128,2,512]{0,2,1:T(8,128)(2,1)S(1)} %collective-permute-done.1), channel_id=1, source_target_pairs={{0,1},{1,2},{2,3},{3,4},{4,5},{5,6},{6,7},{7,8},{8,9},{9,10},{10,1... | collective-permute-start | bytes 786440 | tf_op jit(solution)/shard_map/ppermute | solution.py:18
  40.6 17.9 %collective-permute-start.3 = (bf16[128,2,512]{0,2,1:T(8,128)(2,1)S(1)}, bf16[128,2,512]{0,2,1:T(8,128)(2,1)S(1)}, u32[]{:S(2)}, u32[]{:S(2)}) collective-permute-start(bf16[128,2,512]{0,2,1:T(8,128)(2,1)S(1)} %collective-permute-done.2), channel_id=1, source_target_pairs={{0,1},{1,2},{2,3},{3,4},{4,5},{5,6},{6,7},{7,8},{8,9},{9,10},{10,1... | collective-permute-start | bytes 786440 | tf_op jit(solution)/shard_map/ppermute | solution.py:18
  58.5 12.0 %collective-permute-start.4 = (bf16[128,2,512]{0,2,1:T(8,128)(2,1)S(1)}, bf16[128,2,512]{0,2,1:T(8,128)(2,1)S(1)}, u32[]{:S(2)}, u32[]{:S(2)}) collective-permute-start(bf16[128,2,512]{0,2,1:T(8,128)(2,1)S(1)} %collective-permute-done.3), channel_id=1, source_target_pairs={{0,1},{1,2},{2,3},{3,4},{4,5},{5,6},{6,7},{7,8},{8,9},{9,10},{10,1... | collective-permute-start | bytes 786440 | tf_op jit(solution)/shard_map/ppermute | solution.py:18
  70.5 10.4 %collective-permute-start.5 = (bf16[128,2,512]{0,2,1:T(8,128)(2,1)S(1)}, bf16[128,2,512]{0,2,1:T(8,128)(2,1)S(1)}, u32[]{:S(2)}, u32[]{:S(2)}) collective-permute-start(bf16[128,2,512]{0,2,1:T(8,128)(2,1)S(1)} %collective-permute-done.4), channel_id=1, source_target_pairs={{0,1},{1,2},{2,3},{3,4},{4,5},{5,6},{6,7},{7,8},{8,9},{9,10},{10,1... | collective-permute-start | bytes 786440 | tf_op jit(solution)/shard_map/ppermute | solution.py:18
  80.9 22.1 %collective-permute-start.6 = (bf16[128,2,512]{0,2,1:T(8,128)(2,1)S(1)}, bf16[128,2,512]{0,2,1:T(8,128)(2,1)S(1)}, u32[]{:S(2)}, u32[]{:S(2)}) collective-permute-start(bf16[128,2,512]{0,2,1:T(8,128)(2,1)S(1)} %collective-permute-done.5), channel_id=1, source_target_pairs={{0,1},{1,2},{2,3},{3,4},{4,5},{5,6},{6,7},{7,8},{8,9},{9,10},{10,1... | collective-permute-start | bytes 786440 | tf_op jit(solution)/shard_map/ppermute | solution.py:18
  103.0 21.8 %collective-permute-start.7 = (bf16[128,2,512]{0,2,1:T(8,128)(2,1)S(1)}, bf16[128,2,512]{0,2,1:T(8,128)(2,1)S(1)}, u32[]{:S(2)}, u32[]{:S(2)}) collective-permute-start(bf16[128,2,512]{0,2,1:T(8,128)(2,1)S(1)} %collective-permute-done.6), channel_id=1, source_target_pairs={{0,1},{1,2},{2,3},{3,4},{4,5},{5,6},{6,7},{7,8},{8,9},{9,10},{10,1... | collective-permute-start | bytes 786440 | tf_op jit(solution)/shard_map/ppermute | solution.py:18
  124.8 21.9 %collective-permute-start.8 = (bf16[128,2,512]{0,2,1:T(8,128)(2,1)S(1)}, bf16[128,2,512]{0,2,1:T(8,128)(2,1)S(1)}, u32[]{:S(2)}, u32[]{:S(2)}) collective-permute-start(bf16[128,2,512]{0,2,1:T(8,128)(2,1)S(1)} %collective-permute-done.7), channel_id=1, source_target_pairs={{0,1},{1,2},{2,3},{3,4},{4,5},{5,6},{6,7},{7,8},{8,9},{9,10},{10,1... | collective-permute-start | bytes 786440 | tf_op jit(solution)/shard_map/ppermute | solution.py:18
  146.7 0.7 copy-start
  147.4 9.5 %collective-permute-start.9 = (bf16[128,2,512]{0,2,1:T(8,128)(2,1)S(1)}, bf16[128,2,512]{0,2,1:T(8,128)(2,1)S(1)}, u32[]{:S(2)}, u32[]{:S(2)}) collective-permute-start(bf16[128,2,512]{0,2,1:T(8,128)(2,1)S(1)} %collective-permute-done.8), channel_id=1, source_target_pairs={{0,1},{1,2},{2,3},{3,4},{4,5},{5,6},{6,7},{7,8},{8,9},{9,10},{10,1... | collective-permute-start | bytes 786440 | tf_op jit(solution)/shard_map/ppermute | solution.py:18
  156.9 0.7 copy-start.1
  157.6 9.5 %collective-permute-start.10 = (bf16[128,2,512]{0,2,1:T(8,128)(2,1)S(1)}, bf16[128,2,512]{0,2,1:T(8,128)(2,1)S(1)}, u32[]{:S(2)}, u32[]{:S(2)}) collective-permute-start(bf16[128,2,512]{0,2,1:T(8,128)(2,1)S(1)} %collective-permute-done.9), channel_id=1, source_target_pairs={{0,1},{1,2},{2,3},{3,4},{4,5},{5,6},{6,7},{7,8},{8,9},{9,10},{10,1... | collective-permute-start | bytes 786440 | tf_op jit(solution)/shard_map/ppermute | solution.py:18
  167.1 0.7 copy-start.2
  167.8 9.5 %collective-permute-start.11 = (bf16[128,2,512]{0,2,1:T(8,128)(2,1)S(1)}, bf16[128,2,512]{0,2,1:T(8,128)(2,1)S(1)}, u32[]{:S(2)}, u32[]{:S(2)}) collective-permute-start(bf16[128,2,512]{0,2,1:T(8,128)(2,1)S(1)} %collective-permute-done.10), channel_id=1, source_target_pairs={{0,1},{1,2},{2,3},{3,4},{4,5},{5,6},{6,7},{7,8},{8,9},{9,10},{10,1... | collective-permute-start | bytes 786440 | tf_op jit(solution)/shard_map/ppermute | solution.py:18
  177.3 0.7 copy-start.3
  178.0 9.5 %collective-permute-start.12 = (bf16[128,2,512]{0,2,1:T(8,128)(2,1)S(1)}, bf16[128,2,512]{0,2,1:T(8,128)(2,1)S(1)}, u32[]{:S(2)}, u32[]{:S(2)}) collective-permute-start(bf16[128,2,512]{0,2,1:T(8,128)(2,1)S(1)} %collective-permute-done.11), channel_id=1, source_target_pairs={{0,1},{1,2},{2,3},{3,4},{4,5},{5,6},{6,7},{7,8},{8,9},{9,10},{10,1... | collective-permute-start | bytes 786440 | tf_op jit(solution)/shard_map/ppermute | solution.py:18
  187.5 0.7 copy-start.4
  188.2 9.5 %collective-permute-start.13 = (bf16[128,2,512]{0,2,1:T(8,128)(2,1)S(1)}, bf16[128,2,512]{0,2,1:T(8,128)(2,1)S(1)}, u32[]{:S(2)}, u32[]{:S(2)}) collective-permute-start(bf16[128,2,512]{0,2,1:T(8,128)(2,1)S(1)} %collective-permute-done.12), channel_id=1, source_target_pairs={{0,1},{1,2},{2,3},{3,4},{4,5},{5,6},{6,7},{7,8},{8,9},{9,10},{10,1... | collective-permute-start | bytes 786440 | tf_op jit(solution)/shard_map/ppermute | solution.py:18
  197.6 12.1 %copy-start.5 = (bf16[128,2,512]{0,2,1:T(8,128)(2,1)}, bf16[128,2,512]{0,2,1:T(8,128)(2,1)S(1)}, u32[]{:S(2)}) copy-start(bf16[128,2,512]{0,2,1:T(8,128)(2,1)S(1)} %collective-permute-done.13) | copy-start | bytes 786436
  197.6 9.6 %collective-permute-start.14 = (bf16[128,2,512]{0,2,1:T(8,128)(2,1)S(1)}, bf16[128,2,512]{0,2,1:T(8,128)(2,1)}, u32[]{:S(2)}, u32[]{:S(2)}) collective-permute-start(bf16[128,2,512]{0,2,1:T(8,128)(2,1)S(1)} %collective-permute-done.13), channel_id=1, source_target_pairs={{0,1},{1,2},{2,3},{3,4},{4,5},{5,6},{6,7},{7,8},{8,9},{9,10},{10,1... | collective-permute-start | bytes 786440 | tf_op jit(solution)/shard_map/ppermute | solution.py:18
  207.2 9.8 %collective-permute-start.15 = (bf16[128,2,512]{0,2,1:T(8,128)(2,1)}, bf16[128,2,512]{0,2,1:T(8,128)(2,1)}, u32[]{:S(2)}, u32[]{:S(2)}) collective-permute-start(bf16[128,2,512]{0,2,1:T(8,128)(2,1)} %collective-permute-done.14), channel_id=1, source_target_pairs={{0,1},{1,2},{2,3},{3,4},{4,5},{5,6},{6,7},{7,8},{8,9},{9,10},{10,1... | collective-permute-start | bytes 786440 | tf_op jit(solution)/shard_map/ppermute | solution.py:18
Sparse Core Ops, SparseCore 0:
  10.2 141.4 all-gather.1
where the time goes:
time: 404 us; the launch traced here: 401 us
  waiting for transfers between devices  170 us (42%)
  matrix products  94.7 us (23%)
  other arithmetic  69.7 us (17%)
  starting transfers between devices  30.6 us (8%)
  local copies, waits for them, and re-layouts  20.5 us (5%)
  between operations  13.7 us (3%)
    ppermute x16, waiting for transfers between devices, passed_along(): return lax.ppermute(block, axis, route)  170 us
    dot_general x128, matrix products, one_tile(): jnp.dot(input_classes[nibble_index], weight, preferred_element_type=jnp.f...  44.4 us
    convert_element_type x16, other arithmetic, one_tile(): weight = scaled.reshape(word_rows, tile_width).astype(jnp.bfloat16)  43.1 us
    ppermute x16, starting transfers between devices, passed_along(): return lax.ppermute(block, axis, route)  30.6 us
    sub x4, matrix products, attend(): weights = jnp.where(allowed, jnp.exp(scores - row_max), 0.0)  30.5 us
    dot_general x4, matrix products, attend(): jnp.einsum('hij,jd->hid', rounded, value_rows, preferred_element_type=jnp...  17.8 us
    unnamed x30, local copies, waits for them, and re-layouts  14.9 us
    convert_element_type x16, other arithmetic, one_tile(): lax.dynamic_slice_in_dim(scale_cols, begin, tile_width, 1)  12.3 us
  transfers between devices with their start and end apart: 17, of which 16 were waited for; matrix products, arithmetic and copies ran while one was open for 20% of the time, Pallas kernels for 0%

commit v1 on v0

v1 whole, which is shorter than its diff:
```python
import functools
import math

import jax
import jax.numpy as jnp
from jax import lax
from jax.experimental import pallas as pl
from jax.experimental.pallas import tpu as pltpu
from jax.sharding import PartitionSpec as P

HEADS = 32
KV = 4
HD = 128
GROUP = 128
WINDOW = 2048
PLANE = 8
STEPS = 8
PER_STEP = HEADS // STEPS
LOG2E = 1.4426950408889634
MESH = pl.DeviceIdType.MESH
BF16 = jnp.bfloat16
F32 = jnp.float32

TO_COLUMN, TO_X, TO_Y, PASS_Y, PASS_X, TO_CORE = 0, 1, 2, 3, 4, 5
KINDS = 9


def reordered_hadamard():
    column = jnp.arange(HD, dtype=jnp.int32)
    source = (column % 16) * 8 + column // 16
    common = jnp.bitwise_and(jnp.arange(HD, dtype=jnp.int32)[:, None], source[None, :])
    ones = jnp.zeros((HD, HD), jnp.int32)
    for bit in range(HD.bit_length()):
        ones = ones + jnp.bitwise_and(jnp.right_shift(common, bit), 1)
    return jnp.where(ones % 2 == 0, 1.0, -1.0).astype(BF16)


def kernel(
    n, reach,
    q_ref, kv_ref, sign_ref, had_ref, codes_ref, scales_ref, out_ref,
    kvbuf, cbuf, rot, bias, local_sem, kv_send, kv_recv, c_send, c_recv,
):
    rows = q_ref.shape[0]
    cols = codes_ref.shape[1]
    planes = n // PLANE
    back = -(-reach // PLANE)
    me = lax.axis_index("seq")
    z = me // PLANE
    p = me % PLANE
    core, x, y = p % 2, (p // 2) % 2, p // 4
    dx, dy, dc = 2 - 4 * x, 4 - 8 * y, 1 - 2 * core
    px, py, pd = p + dx, p + dy, p + dx + dy

    def column(d):
        return lax.rem(z + d, planes) * PLANE + p

    barrier = pltpu.get_barrier_semaphore()
    peers = [column(d) for d in range(1, planes)] + [me + dx, me + dy, me + dc]
    for peer in peers:
        pl.semaphore_signal(barrier, inc=1, device_id={"seq": peer}, device_id_type=MESH)
    own_kv = pltpu.make_async_copy(kv_ref, kvbuf.at[back * PLANE + p], local_sem.at[0])
    own_codes = pltpu.make_async_copy(codes_ref, cbuf.at[me], local_sem.at[1])
    own_kv.start()
    own_codes.start()

    class Item:
        def __init__(self, buf, base, send, recv):
            self.buf, self.base, self.send, self.recv = buf, base, send, recv
            self.half = buf.shape[1] // 2

        def move(self, kind, d, q, target, part=None, source=None, to=None):
            block = self.buf.at[self.base(d) + q]
            if part is not None:
                block = self.buf.at[self.base(d) + q, pl.ds(part * self.half, self.half)]
            return pltpu.make_async_remote_copy(
                src_ref=block if source is None else source,
                dst_ref=block,
                send_sem=self.send.at[kind, d],
                recv_sem=self.recv.at[kind, d],
                device_id={"seq": target},
                device_id_type=MESH,
            )

        def to_column(self, d, source):
            return self.move(TO_COLUMN, d, p, column(d), source=source)

        def to_x(self, d):
            return self.move(TO_X, d, p, me + dx)

        def to_y(self, d):
            return self.move(TO_Y, d, p, me + dy)

        def pass_y(self, d):
            return self.move(PASS_Y, d, px, me + dy, part=0)

        def pass_x(self, d):
            return self.move(PASS_X, d, py, me + dx, part=1)

        def to_core(self, d, which):
            return self.move(TO_CORE + which, d, (p, px, py, pd)[which], me + dc)

        def stage1(self, d):
            self.to_x(d).start()
            self.to_y(d).start()
            self.to_core(d, 0).start()

        def stage2(self, d):
            self.to_x(d).wait_recv()
            self.pass_y(d).start()
            self.to_core(d, 1).start()
            self.to_y(d).wait_recv()
            self.pass_x(d).start()
            self.to_core(d, 2).start()

        def stage3(self, d):
            self.pass_y(d).wait_recv()
            self.pass_x(d).wait_recv()
            self.to_core(d, 3).start()

        def stage4(self, d):
            for which in range(4):
                self.to_core(d, which).wait_recv()

        def sent(self, d):
            for copy in (self.to_x(d), self.to_y(d), self.pass_y(d), self.pass_x(d)):
                copy.wait_send()
            for which in range(4):
                self.to_core(d, which).wait_send()

    kv = Item(kvbuf, lambda d: (back - d) * PLANE, kv_send, kv_recv)
    codes = Item(cbuf, lambda d: lax.rem(z + planes - d, planes) * PLANE, c_send, c_recv)

    own_kv.wait()
    own_codes.wait()
    pl.semaphore_wait(barrier, len(peers))

    def kv_out(d):
        block = kvbuf.at[back * PLANE + p]
        return pltpu.make_async_remote_copy(
            src_ref=block, dst_ref=kvbuf.at[(back - d) * PLANE + p],
            send_sem=kv_send.at[TO_COLUMN, d], recv_sem=kv_recv.at[TO_COLUMN, d],
            device_id={"seq": column(d)}, device_id_type=MESH,
        )

    def codes_out(d):
        return pltpu.make_async_remote_copy(
            src_ref=cbuf.at[me], dst_ref=cbuf.at[me],
            send_sem=c_send.at[TO_COLUMN, d], recv_sem=c_recv.at[TO_COLUMN, d],
            device_id={"seq": column(d)}, device_id_type=MESH,
        )

    def there(d):
        return z - d >= 0

    near = [d for d in range(1, back + 1) if d < planes]
    for d in near:
        @pl.when(z + d < planes)
        def _():
            kv_out(d).start()
    kv.stage1(0)
    for d in range(1, planes):
        codes_out(d).start()

    for d in range(1, back + 1):
        @pl.when(jnp.logical_not(there(d)))
        def _():
            first = (back - d) * PLANE
            kvbuf[first:first + PLANE] = jnp.zeros((PLANE,) + kvbuf.shape[1:], kvbuf.dtype)

    window_blocks = reach + 1
    first_block = back * PLANE + p - reach
    keys = window_blocks * rows
    query = lax.broadcasted_iota(jnp.int32, (rows, keys), 0)
    key = lax.broadcasted_iota(jnp.int32, (rows, keys), 1) - reach * rows
    gap = query - key
    allowed = (gap >= 0) & (gap < WINDOW) & (key + me * rows >= 0)
    bias[...] = jnp.where(allowed, 0.0, -jnp.inf).astype(F32)

    for d in range(0, back + 1):
        if d in near:
            @pl.when(there(d))
            def _():
                kv_out(d).wait_recv()
                kv.stage1(d)
        if d >= 1 and (d == 1 or d - 1 in near):
            @pl.when(there(d - 1))
            def _():
                kv.stage2(d - 1)
    levels = [0] + near
    @pl.when(there(levels[-1]))
    def _():
        kv.stage2(levels[-1])
    codes.stage1(0)
    for d in levels:
        @pl.when(there(d))
        def _():
            kv.stage3(d)
    for d in levels:
        @pl.when(there(d))
        def _():
            kv.stage4(d)

    def event(j):
        @pl.when(j < planes)
        def _():
            codes_out(j).wait_recv()
            codes.stage1(j)

        @pl.when(j - 1 < planes)
        def _():
            codes.stage2(j - 1)

    def third(d):
        @pl.when(d < planes)
        def _():
            codes.stage3(d)

    def attend(t, carry):
        start = pl.multiple_of(t * (PER_STEP * HD), PER_STEP * HD)
        group = (t * PER_STEP) // (HEADS // KV)
        q = q_ref[:, pl.ds(start, PER_STEP * HD)]
        q = jnp.concatenate([q[:, k * HD:(k + 1) * HD] for k in range(PER_STEP)], axis=0)
        key_lane = pl.multiple_of(group * HD, HD)
        value_lane = pl.multiple_of(group * HD + KV * HD, HD)
        k_rows = kvbuf[pl.ds(first_block, window_blocks), :, pl.ds(key_lane, HD)].reshape(keys, HD)
        v_rows = kvbuf[pl.ds(first_block, window_blocks), :, pl.ds(value_lane, HD)].reshape(keys, HD)
        scores = lax.dot_general(q, k_rows, (((1,), (1,)), ((), ())), preferred_element_type=F32)
        scores = scores.reshape(PER_STEP, rows, keys) * (LOG2E / math.sqrt(HD)) + bias[...][None]
        top = jnp.max(scores, axis=-1, keepdims=True)
        weights = jnp.exp2(scores - top)
        total = jnp.sum(weights, axis=-1, keepdims=True)
        rounded = weights.astype(BF16).reshape(PER_STEP * rows, keys)
        weighted = jnp.dot(rounded, v_rows, preferred_element_type=F32)
        weighted = weighted.reshape(PER_STEP, rows, HD) / total
        signed = weighted * sign_ref[t].astype(F32)[:, None, :]
        signed = signed.reshape(PER_STEP * rows, HD)
        high = signed.astype(BF16)
        low = (signed - high.astype(F32)).astype(BF16)
        mixed = jnp.dot(high, had_ref[...], preferred_element_type=F32)
        mixed = mixed + jnp.dot(low, had_ref[...], preferred_element_type=F32)
        mixed = (mixed * (1.0 / math.sqrt(HD))).astype(BF16)
        for k in range(PER_STEP):
            lanes = pl.ds(pl.multiple_of(start + k * HD, HD), HD)
            rot[:, lanes] = mixed[k * rows:(k + 1) * rows]

        @pl.when(t == 2)
        def _():
            event(1)

        @pl.when(t == 5)
        def _():
            event(2)
            third(0)

        return carry

    lax.fori_loop(0, STEPS, attend, 0)

    chunk_heads = 8
    words = GROUP // 8

    def project(s):
        lanes = pl.ds(pl.multiple_of(s * cols, cols), cols)
        scale = scales_ref[:, lanes]
        acc = jnp.zeros((rows, cols), F32)
        for chunk in range(HEADS // chunk_heads):
            parts = []
            for h in range(chunk * chunk_heads, (chunk + 1) * chunk_heads):
                word = cbuf[s, h * words:(h + 1) * words, :] ^ jnp.int32(-2004318072)
                factor = jnp.broadcast_to(scale[h:h + 1, :], (words, cols))
                for k in range(8):
                    code = jnp.right_shift(jnp.left_shift(word, 28 - 4 * k), 28)
                    parts.append(code.astype(F32).astype(BF16) * factor)
            weight = jnp.concatenate(parts, axis=0)
            piece = rot[:, chunk * chunk_heads * HD:(chunk + 1) * chunk_heads * HD]
            acc = acc + jnp.dot(piece, weight, preferred_element_type=F32)
        out_ref[:, lanes] = acc.astype(BF16)

    def finish(j, carry):
        event(j)
        third(j - 2)
        level = j - 3
        codes.stage4(level)
        base = codes.base(level)

        def one(q, c):
            project(base + q)
            return c

        return lax.fori_loop(0, PLANE, one, carry)

    lax.fori_loop(3, planes + 3, finish, 0)

    for d in near:
        @pl.when(z + d < planes)
        def _():
            kv_out(d).wait_send()
    for d in levels:
        @pl.when(there(d))
        def _():
            kv.sent(d)
    for d in range(1, planes):
        codes_out(d).wait_send()

    def sent(d, carry):
        codes.sent(d)
        return carry

    lax.fori_loop(0, planes, sent, 0)


def on_device(queries, keys_values, head_signs, out_codes, out_scales):
    n = lax.axis_size("seq")
    rows = queries.shape[0]
    reach = (WINDOW + rows - 2) // rows
    back = -(-reach // PLANE)
    planes = n // PLANE
    word_rows, cols = out_codes.shape
    vmem = pl.BlockSpec(memory_space=pltpu.VMEM)
    dma = pltpu.SemaphoreType.DMA
    return pl.pallas_call(
        functools.partial(kernel, n, reach),
        out_shape=jax.ShapeDtypeStruct((rows, n * cols), BF16),
        in_specs=[vmem] * 6,
        out_specs=vmem,
        scratch_shapes=[
            pltpu.VMEM(((back + 1) * PLANE, rows, 2 * KV * HD), BF16),
            pltpu.VMEM((n, word_rows, cols), jnp.int32),
            pltpu.VMEM((rows, HEADS * HD), BF16),
            pltpu.VMEM((rows, (reach + 1) * rows), F32),
            dma((2,)),
            dma((KINDS, back + 1)),
            dma((KINDS, back + 1)),
            dma((KINDS, planes)),
            dma((KINDS, planes)),
        ],
        compiler_params=pltpu.CompilerParams(
            collective_id=0, has_side_effects=True, vmem_limit_bytes=64 * 1000 * 1000
        ),
    )(
        queries,
        keys_values.reshape(rows, 2 * KV * HD),
        head_signs.reshape(STEPS, PER_STEP, HD),
        reordered_hadamard(),
        out_codes,
        out_scales,
    )


def solution(mesh):
    return jax.shard_map(
        on_device,
        mesh=mesh,
        in_specs=(
            P(("groups", "seq"), None),
            P(("groups", "seq"), None, None),
            P(),
            P(None, "seq"),
            P(),
        ),
        out_specs=P(("groups", "seq"), None),
        check_vma=False,
    )
```

time: 404 us -> 137 us (0.34)
  waiting for transfers between devices: 170 us -> 0 us
  Pallas kernels: 0 us -> 131 us
  matrix products: 94.7 us -> 0 us
  other arithmetic: 69.7 us -> 0.7 us
  starting transfers between devices: 30.6 us -> 0 us
  local copies, waits for them, and re-layouts: 20.5 us -> 4.78 us
  between operations: 13.7 us -> 0.01 us
    ppermute x16 -> x0, waiting for transfers between devices: 170 us -> none  [passed_along(): return lax.ppermute(block, axis, route)]
    pallas_call x0 -> x1, Pallas kernels: none -> 131 us  [on_device(): pl.pallas_call(functools.partial(kernel, n, reach), out_shape=jax.ShapeDt...]
    dot_general x133 -> x0, matrix products: 64.3 us -> none  [the longest x128 44.4 us: one_tile(): jnp.dot(input_classes[nibble_index], weight, preferred_element_type=jnp.f...]
    convert_element_type x33 -> x1, other arithmetic: 56.8 us -> 0.69 us  [reordered_hadamard(): return jnp.where(ones % 2 == 0, 1.0, -1.0).astype(BF16)]
    ppermute x16 -> x0, starting transfers between devices: 30.6 us -> none  [passed_along(): return lax.ppermute(block, axis, route)]
    sub x4 -> x0, matrix products: 30.5 us -> none  [attend(): weights = jnp.where(allowed, jnp.exp(scores - row_max), 0.0)]
    unnamed x30 -> x2, local copies, waits for them, and re-layouts: 14.9 us -> 4.78 us
    broadcast_in_dim x5 -> x0, other arithmetic: 9.46 us -> none  [the longest x4 9.45 us: attend(): weights = jnp.where(allowed, jnp.exp(scores - row_max), 0.0)]
  transfers between devices with their start and end apart: 17 -> 0, of which waited for: 16 -> 0; matrix products, arithmetic and copies ran while one was open for 20% -> 0% of each run, Pallas kernels for 0% -> 0%
where the time goes in v1:
time: 137 us
  Pallas kernels  131 us (96%)
  local copies, waits for them, and re-layouts  4.78 us (3%)
    pallas_call x1, Pallas kernels, on_device(): pl.pallas_call(functools.partial(kernel, n, reach), out_shape=jax.ShapeDt...  131 us
    unnamed x2, local copies, waits for them, and re-layouts  4.78 us

profile of v1, /device:TPU:16, one launch (start us, length us, event | category | flops | bytes accessed | tf_op | source)
XLA Modules:
  0.0 136.5 jit_solution(14437978981418599020)
XLA Ops:
  0.0 0.7 select_convert_fusion.had_ref
  0.7 1.7 %copy.6 = bf16[16,8,2,512]{3,1,2,0:T(8,128)(2,1)} copy(bf16[16,8,2,512]{3,2,1,0:T(2,128)(2,1)} %bitcast.4) | data formatting | bytes 524288
  2.4 131.0 %shard_map.55 = bf16[128,8192]{1,0:T(8,128)(2,1)} custom-call(bf16[128,4096]{1,0:T(8,128)(2,1)} %q_ref.1, bf16[128,1024]{1,0:T(8,128)(2,1)} %bitcast.3, s32[8,4,128]{2,1,0:T(4,128)} %bitcast.5, bf16[128,128]{1,0:T(8,128)(2,1)} %select_convert_fusion.had_ref, s32[512,256]{1,0:T(8,128)} %codes_ref.1, bf16[32,8192]{1,0:T(8,128)(2,1)} %scales_ref.1), custom_call_target="tpu_custom_call" | custom-call | tf_op jit(solution)/shard_map/pallas_call | solution.py:321
  133.4 3.1 %copy.8 = bf16[128,8192]{1,0:T(8,128)(2,1)} copy(bf16[128,8192]{1,0:T(8,128)(2,1)} %shard_map.55) | data formatting | bytes 4194304
  (1 shorter events, 0.0 us)

commit v2 on v1

--- a/solution.py
+++ b/solution.py
@@ -276,20 +276,32 @@
             acc = acc + jnp.dot(piece, weight, preferred_element_type=F32)
         out_ref[:, lanes] = acc.astype(BF16)
 
+    def project_some(d, low, high):
+        def one(q, c):
+            which = q // 2
+            project(codes.base(d) + p + (which % 2) * dx + (which // 2) * dy + (q % 2) * dc)
+            return c
+
+        lax.fori_loop(low, high, one, 0)
+
     def finish(j, carry):
+        @pl.when(j - 3 < planes)
+        def _():
+            for which in range(3):
+                codes.to_core(j - 3, which).wait_recv()
+            project_some(j - 3, 0, 6)
+
         event(j)
-        third(j - 2)
-        level = j - 3
-        codes.stage4(level)
-        base = codes.base(level)
-
-        def one(q, c):
-            project(base + q)
-            return c
-
-        return lax.fori_loop(0, PLANE, one, carry)
-
-    lax.fori_loop(3, planes + 3, finish, 0)
+
+        @pl.when(j >= 4)
+        def _():
+            third(j - 3)
+            codes.to_core(j - 4, 3).wait_recv()
+            project_some(j - 4, 6, 8)
+
+        return carry
+
+    lax.fori_loop(3, planes + 4, finish, 0)
 
     for d in near:
         @pl.when(z + d < planes)

time: 137 us -> 129 us (0.942)
  Pallas kernels: 131 us -> 123 us
    pallas_call x1, Pallas kernels: 131 us -> 123 us  [on_device(): pl.pallas_call(functools.partial(kernel, n, reach), out_shape=jax.ShapeDt...]
where the time goes in v2:
time: 129 us; the launch traced here: 128 us
  Pallas kernels  123 us (95%)
  local copies, waits for them, and re-layouts  4.78 us (4%)
    pallas_call x1, Pallas kernels, on_device(): pl.pallas_call(functools.partial(kernel, n, reach), out_shape=jax.ShapeDt...  123 us
    unnamed x2, local copies, waits for them, and re-layouts  4.78 us

profile of v2, /device:TPU:16, one launch (start us, length us, event | category | flops | bytes accessed | tf_op | source)
XLA Modules:
  0.0 128.2 jit_solution(2958016778470971778)
XLA Ops:
  0.0 0.7 select_convert_fusion.had_ref
  0.7 1.7 %copy.6 = bf16[16,8,2,512]{3,1,2,0:T(8,128)(2,1)} copy(bf16[16,8,2,512]{3,2,1,0:T(2,128)(2,1)} %bitcast.4) | data formatting | bytes 524288
  2.4 122.7 %shard_map.55 = bf16[128,8192]{1,0:T(8,128)(2,1)} custom-call(bf16[128,4096]{1,0:T(8,128)(2,1)} %q_ref.1, bf16[128,1024]{1,0:T(8,128)(2,1)} %bitcast.3, s32[8,4,128]{2,1,0:T(4,128)} %bitcast.5, bf16[128,128]{1,0:T(8,128)(2,1)} %select_convert_fusion.had_ref, s32[512,256]{1,0:T(8,128)} %codes_ref.1, bf16[32,8192]{1,0:T(8,128)(2,1)} %scales_ref.1), custom_call_target="tpu_custom_call" | custom-call | tf_op jit(solution)/shard_map/pallas_call | solution.py:333
  125.1 3.1 %copy.8 = bf16[128,8192]{1,0:T(8,128)(2,1)} copy(bf16[128,8192]{1,0:T(8,128)(2,1)} %shard_map.55) | data formatting | bytes 4194304
  (1 shorter events, 0.0 us)
